TPU v7x, 32 devices: a whole 2x2x4 slice. The times are simulated.
32 devices in a mesh: seq: 8 (over y, x, core), tp: 4 (over z).
Axes of the slice: x: 2, y: 2, z: 4, core: 2. Of those that a mesh axis runs over, the one named last changes fastest.
Arguments:
- x_input: bfloat16 [8192, 8192], P('seq', 'tp'), may hold values from -6 to 6
- bc_input: bfloat16 [8192, 2048], P('seq', 'tp'), may hold values from -3 to 3
- z_gate: bfloat16 [8192, 8192], P('seq', 'tp'), may hold values from -6 to 6
- dt_input: bfloat16 [128, 8192], P('tp', 'seq'), may hold values from -3.4 to 3.4
- conv_weight_x: bfloat16 [4, 8192], P(None, 'tp'), may hold values from -3 to 3
- conv_weight_bc: bfloat16 [4, 2048], P(None, 'tp'), may hold values from -3 to 3
- conv_bias_x: float32 [8192], P('tp'), may hold values from -3 to 3
- conv_bias_bc: float32 [2048], P('tp'), may hold values from -3 to 3
- dt_bias: float32 [128], P('tp'), may hold values from -1 to 0.5
- decay_log: float32 [128], P('tp'), may hold values from -12 to -3.3
- skip_scale: float32 [128], P('tp'), may hold values from 0.5 to 2
- norm_gain: float32 [8192], P('tp'), may hold values from 0.25 to 1.75
Outputs:
- layer_out: bfloat16 [8192, 8192], P('seq', 'tp')
All inputs are finite; a program needn't handle non-finite values.
Results may differ from a plain program's by a relative error of at most 0.0048.
Values may be sent and summed in bfloat16 or wider, within the bound.
A program may use at most 128 MiB of HBM per device.

v0:
```python
import jax
import jax.numpy as jnp
from jax import lax
from jax.sharding import PartitionSpec as P

HEAD_DIM = 64
STATE = 128
SPAN = 256
DI = 8192


epsilon = 1e-05


def from_behind(value, axis, steps):
    count = lax.axis_size(axis)
    initial, last = (max(0, -steps), min(count, count - steps))
    return lax.ppermute(value, axis, [(source, source + steps) for source in range(initial, last)])


def prefix(part, axis, combine, identity):
    place = lax.axis_index(axis)
    gathered = jax.tree.map(lambda a: lax.all_gather(a, axis), part)
    state = jax.tree.map(lambda a, e: jnp.zeros_like(a) + jnp.asarray(e, a.dtype), part, identity)

    def one(turn, state):
        return combine(
            state, jax.tree.map(lambda a: lax.dynamic_index_in_dim(a, turn, 0, False), gathered)
        )

    return lax.fori_loop(0, place, one, state)


def causal_conv(padded, weight, bias_row):
    length = padded.shape[0] - 3
    total = jnp.zeros((length, padded.shape[1]), jnp.float32) + bias_row[None, :]
    for offset in range(4):
        total = (
            total
            + padded[offset : offset + length].astype(jnp.float32)
            * weight[offset].astype(jnp.float32)[None, :]
        )
    return jax.nn.silu(total).astype(jnp.bfloat16)


def span_local(x_block, bc_block, dt_block, decay_block):
    block_len = x_block.shape[0]
    heads = x_block.shape[1]
    groups = bc_block.shape[1]
    group_heads = heads // groups
    cum_decay = jnp.cumsum(decay_block, axis=1)
    b_part = bc_block[:, :, 0, :]
    c_part = bc_block[:, :, 1, :]
    scores = jnp.einsum("ign,jgn->gij", c_part, b_part, preferred_element_type=jnp.float32)
    causal = jnp.arange(block_len)[:, None] >= jnp.arange(block_len)[None, :]
    spread = jnp.where(causal[None], cum_decay[:, :, None] - cum_decay[:, None, :], -jnp.inf)
    weights = jnp.exp(spread) * dt_block[:, None, :]
    mixing = (
        (weights.reshape(groups, group_heads, block_len, block_len) * scores[:, None])
        .reshape(heads, block_len, block_len)
        .astype(jnp.bfloat16)
    )
    y_intra = jnp.einsum("hij,jhp->ihp", mixing, x_block, preferred_element_type=jnp.float32)
    to_end = jnp.exp(cum_decay[:, -1:] - cum_decay) * dt_block
    weighted = (
        (
            to_end.reshape(groups, group_heads, block_len)[:, :, :, None]
            * b_part.transpose(1, 0, 2)[:, None]
        )
        .reshape(heads, block_len, b_part.shape[2])
        .astype(jnp.bfloat16)
    )
    span_state = jnp.einsum("hjn,jhp->hnp", weighted, x_block, preferred_element_type=jnp.float32)
    return (y_intra, span_state, cum_decay)


def join(earlier, later):
    return (earlier[0] + later[0], jnp.exp(later[0])[:, None, None] * earlier[1] + later[1])


def local(
    x_input,
    bc_input,
    z_gate,
    dt_input,
    conv_weight_x,
    conv_weight_bc,
    conv_bias_x,
    conv_bias_bc,
    dt_bias,
    decay_log,
    skip_scale,
    norm_gain,
):
    rim_x, rim_bc = from_behind((x_input[-3:], bc_input[-3:]), "seq", 1)
    x_conv = causal_conv(jnp.concatenate([rim_x, x_input], 0), conv_weight_x, conv_bias_x)
    bc_conv = causal_conv(jnp.concatenate([rim_bc, bc_input], 0), conv_weight_bc, conv_bias_bc)
    tokens = x_input.shape[0]
    heads = dt_input.shape[0]
    groups = bc_input.shape[1] // (2 * STATE)
    blocks = tokens // SPAN
    step_size = jax.nn.softplus(dt_input.astype(jnp.float32) + dt_bias[:, None])
    log_decay = -jnp.exp(decay_log)[:, None] * step_size
    x_blocks = x_conv.reshape(blocks, SPAN, heads, HEAD_DIM)
    bc_blocks = bc_conv.reshape(blocks, SPAN, groups, 2, STATE)
    dt_blocks = step_size.reshape(heads, blocks, SPAN).transpose(1, 0, 2)
    decay_blocks = log_decay.reshape(heads, blocks, SPAN).transpose(1, 0, 2)

    def advance(carried, pieces):
        x_block, bc_block, dt_block, decay_block = pieces
        y_intra, span_state, cum_decay = span_local(x_block, bc_block, dt_block, decay_block)
        updated = jnp.exp(cum_decay[:, -1])[:, None, None] * carried + span_state
        return (updated, (y_intra, carried, cum_decay))

    initial = jnp.zeros((heads, STATE, HEAD_DIM), jnp.float32)
    local_end, (y_intra, local_start, cum_decay) = lax.scan(
        advance, initial, (x_blocks, bc_blocks, dt_blocks, decay_blocks)
    )
    block_total = cum_decay[:, :, -1]
    device_total = jnp.sum(block_total, axis=0)
    before = jnp.cumsum(block_total, axis=0) - block_total
    local_pair = (device_total, local_end)
    identity = (jnp.zeros_like(device_total), jnp.zeros_like(local_end))
    incoming = prefix(local_pair, "seq", join, identity)
    start = (local_start + jnp.exp(before)[:, :, None, None] * incoming[1][None]).astype(
        jnp.bfloat16
    )
    c_part = bc_blocks[:, :, :, 1, :]
    grouped = start.reshape(blocks, groups, heads // groups, STATE, HEAD_DIM)
    product = jnp.einsum(
        "kign,kgrnp->kigrp", c_part, grouped, preferred_element_type=jnp.float32
    ).reshape(blocks, SPAN, heads, HEAD_DIM)
    y_state = jnp.exp(cum_decay).transpose(0, 2, 1)[:, :, :, None] * product
    mixed = (y_intra + y_state).reshape(tokens, heads, HEAD_DIM) + skip_scale[
        None, :, None
    ] * x_conv.reshape(tokens, heads, HEAD_DIM).astype(jnp.float32)
    gated = mixed.reshape(tokens, heads * HEAD_DIM) * jax.nn.silu(z_gate.astype(jnp.float32))
    partial_sum = jnp.sum(gated * gated, axis=1)
    total_sum = lax.psum(partial_sum, "tp")
    factor = lax.rsqrt(total_sum / DI + epsilon)
    return (gated * factor[:, None] * norm_gain[None, :]).astype(jnp.bfloat16)


def solution(mesh):
    in_specs = (
        P("seq", "tp"),
        P("seq", "tp"),
        P("seq", "tp"),
        P("tp", "seq"),
        P(None, "tp"),
        P(None, "tp"),
        P("tp"),
        P("tp"),
        P("tp"),
        P("tp"),
        P("tp"),
        P("tp"),
    )
    out_specs = P("seq", "tp")
    return jax.shard_map(local, mesh=mesh, in_specs=in_specs, out_specs=out_specs, check_vma=False)
```

profile of v0, /device:TPU:7, one launch (start us, length us, event | category | flops | bytes accessed | tf_op | source)
XLA Modules:
  0.0 282.3 jit_solution(9640474491370032401)
XLA Ops:
  15.1 6.5 %copy.58 = bf16[1024,2048]{0,1:T(8,128)(2,1)} copy(bf16[1024,2048]{1,0:T(8,128)(2,1)} %param.16) | data formatting | bytes 8388608 | tf_op args[0]
  24.4 18.1 %multiply_convert_fusion.1 = bf16[1024,2048]{0,1:T(8,128)(2,1)} fusion(bf16[1024,2048]{0,1:T(8,128)(2,1)} %copy.58, bf16[3,2048]{0,1:T(8,128)(2,1)} %collective-permute-done.1, f32[2048]{0:T(1024)S(1)} %bitcast.141, f32[2048]{0:T(1024)S(1)} %bitcast.142, f32[2048]{0:T(1024)S(1)} %bitcast.140, f32[2048]{0:T(1024)S(1)} %bitcast.139, f32[2048]{0:T(1024)S(1)} %copy-done.6), kind=kLoop, calls=%fused_computation.41 | loop fusion | flops 54525952 | bytes 8441856 | tf_op jit(solution)/shard_map/convert_element_type | solution.py:43
  42.5 7.8 %reshape.179 = bf16[4,256,32,64]{1,0,3,2:T(4,128)(2,1)} reshape(bf16[1024,2048]{0,1:T(8,128)(2,1)} %multiply_convert_fusion.1) | data formatting | bytes 8388608 | tf_op jit(solution)/shard_map/reshape | solution.py:104
  50.3 4.9 %copy.63 = bf16[4,256,32,64]{1,3,2,0:T(8,128)(2,1)} copy(bf16[4,256,32,64]{1,0,3,2:T(4,128)(2,1)} %reshape.179) | data formatting | bytes 8388608
  55.2 56.3 %while.30 = (s32[]{:T(128)}, f32[32,128,64]{1,2,0:T(8,128)S(1)}, f32[4,256,32,64]{1,3,2,0:T(8,128)}, f32[4,32,128,64]{2,3,1,0:T(8,128)}, f32[4,32,256]{2,1,0:T(8...) while((s32[]{:T(128)}, f32[32,128,64]{1,2,0:T(8,128)S(1)}, ...), condition=%wide.region_3.4_spmd.clone, body=%wide.region_0.3_spmd.clone.sunk | while | flops 451051616 | bytes 24975120 | solution.py:116
  60.0 4.0 %bitcast_dynamic-update-slice_fusion.4 = f32[4,256,32,64]{1,3,2,0:T(8,128)} fusion(f32[4,256,32,64]{1,3,2,0:T(8,128)} %get-tuple-element.339, s32[]{:T(128)} %get-tuple-element.337, bf16[32,256,256]{2,1,0:T(8,128)(2,1)S(1)} %fusion.42, bf16[4,256,32,64]{1,3,2,0:T(8,128)(2,1)} %get-tuple-element.357), kind=kOutput, calls=%fused_computation.7.clone.1 | convolution fusion | flops 268435456 | bytes 7341056 | tf_op jit(solution)/shard_map/while/body/eval_jaxpr/hij,jhp->ihp/dot_general | solution.py:63
  71.8 2.3 fusion.42
  74.1 3.9 %bitcast_dynamic-update-slice_fusion.4 = f32[4,256,32,64]{1,3,2,0:T(8,128)} fusion(f32[4,256,32,64]{1,3,2,0:T(8,128)} %get-tuple-element.339, s32[]{:T(128)} %get-tuple-element.337, bf16[32,256,256]{2,1,0:T(8,128)(2,1)S(1)} %fusion.42, bf16[4,256,32,64]{1,3,2,0:T(8,128)(2,1)} %get-tuple-element.357), kind=kOutput, calls=%fused_computation.7.clone.1 | convolution fusion | flops 268435456 | bytes 7341056 | tf_op jit(solution)/shard_map/while/body/eval_jaxpr/hij,jhp->ihp/dot_general | solution.py:63
  85.8 2.3 fusion.42
  88.2 4.0 %bitcast_dynamic-update-slice_fusion.4 = f32[4,256,32,64]{1,3,2,0:T(8,128)} fusion(f32[4,256,32,64]{1,3,2,0:T(8,128)} %get-tuple-element.339, s32[]{:T(128)} %get-tuple-element.337, bf16[32,256,256]{2,1,0:T(8,128)(2,1)S(1)} %fusion.42, bf16[4,256,32,64]{1,3,2,0:T(8,128)(2,1)} %get-tuple-element.357), kind=kOutput, calls=%fused_computation.7.clone.1 | convolution fusion | flops 268435456 | bytes 7341056 | tf_op jit(solution)/shard_map/while/body/eval_jaxpr/hij,jhp->ihp/dot_general | solution.py:63
  102.2 3.9 %bitcast_dynamic-update-slice_fusion.4 = f32[4,256,32,64]{1,3,2,0:T(8,128)} fusion(f32[4,256,32,64]{1,3,2,0:T(8,128)} %get-tuple-element.339, s32[]{:T(128)} %get-tuple-element.337, bf16[32,256,256]{2,1,0:T(8,128)(2,1)S(1)} %fusion.42, bf16[4,256,32,64]{1,3,2,0:T(8,128)(2,1)} %get-tuple-element.357), kind=kOutput, calls=%fused_computation.7.clone.1 | convolution fusion | flops 268435456 | bytes 7341056 | tf_op jit(solution)/shard_map/while/body/eval_jaxpr/hij,jhp->ihp/dot_general | solution.py:63
  112.6 6.4 %copy.68 = bf16[1024,2048]{0,1:T(8,128)(2,1)} copy(bf16[1024,2048]{1,0:T(8,128)(2,1)} %param.18) | data formatting | bytes 8388608 | tf_op args[2]
  120.5 3.4 %slice.105 = bf16[4,256,2,1,128]{4,3,2,1,0:T(2,128)(2,1)} slice(bf16[4,256,2,2,128]{4,3,2,1,0:T(2,128)(2,1)} %reshape.178), slice={[0:4], [0:256], [0:2], [1:2], [0:128]} | slice | bytes 1048576 | tf_op jit(solution)/shard_map/slice | solution.py:128
  124.3 13.0 %all-reduce = f32[256]{0:T(256)S(1)} all-reduce(f32[256]{0:T(256)S(1)} %dynamic-update-slice), channel_id=2, replica_groups=mesh['seq'=8,'tp'=4] {'seq'}, use_global_device_ids=true, to_apply=%add | all-reduce | flops 256 | bytes 2048
  137.5 32.2 %all-gather.4.cloned.1.call-done = f32[256,128,64]{1,2,0:T(8,128)} async-done(((f32[32,128,64]{1,2,0:T(8,128)}), f32[256,128,64]{1,2,0:T(8,128)}) %all-gather.4.cloned.1.call-update) | async-done | bytes 8388624 | tf_op jit(solution)/shard_map/all_gather | solution.py:23
  171.3 35.8 %while.29 = (s32[]{:T(128)}, f32[32,128,64]{2,1,0:T(8,128)}, s32[]{:T(128)}, f32[8,32]{1,0:T(8,128)S(1)}, f32[8,32,128,64]{2,3,1,0:T(8,128)}, /*index=5*/s32[]{:T(128)}, s32[]{:T(128)}, s32[]{:T(128)}) while((s32[]{:T(128)}, f32[32,128,64]{2,1,0:T(8,128)}, s32[]{:T(128)}, f32[8,32]{1,0:T(8,128)S(1)}, f32[8,32,128,64]{2,3,1,0:T(8,128)}, ...), condition=%wide.region_7.8_spmd, body=%wide.region_6.7_spmd.sunk | while | flops 524293 | bytes 7340543 | solution.py:31
  173.2 3.2 %bitcast_add_fusion.2 = f32[32,128,64]{2,1,0:T(8,128)} fusion(f32[1,32,128,64]{3,2,1,0:T(8,128)S(1)} %copy.97, f32[32,128,64]{2,1,0:T(8,128)} %get-tuple-element.370, f32[32]{0:T(128)S(1)} %exponential_bitcast_fusion.3), kind=kLoop, calls=%fused_computation.clone.1 | loop fusion | flops 524288 | bytes 3145856 | tf_op jit(solution)/shard_map/while/body/add | solution.py:78
  178.3 3.2 %bitcast_add_fusion.2 = f32[32,128,64]{2,1,0:T(8,128)} fusion(f32[1,32,128,64]{3,2,1,0:T(8,128)S(1)} %copy.97, f32[32,128,64]{2,1,0:T(8,128)} %get-tuple-element.370, f32[32]{0:T(128)S(1)} %exponential_bitcast_fusion.3), kind=kLoop, calls=%fused_computation.clone.1 | loop fusion | flops 524288 | bytes 3145856 | tf_op jit(solution)/shard_map/while/body/add | solution.py:78
  183.4 3.2 %bitcast_add_fusion.2 = f32[32,128,64]{2,1,0:T(8,128)} fusion(f32[1,32,128,64]{3,2,1,0:T(8,128)S(1)} %copy.97, f32[32,128,64]{2,1,0:T(8,128)} %get-tuple-element.370, f32[32]{0:T(128)S(1)} %exponential_bitcast_fusion.3), kind=kLoop, calls=%fused_computation.clone.1 | loop fusion | flops 524288 | bytes 3145856 | tf_op jit(solution)/shard_map/while/body/add | solution.py:78
  188.5 3.2 %bitcast_add_fusion.2 = f32[32,128,64]{2,1,0:T(8,128)} fusion(f32[1,32,128,64]{3,2,1,0:T(8,128)S(1)} %copy.97, f32[32,128,64]{2,1,0:T(8,128)} %get-tuple-element.370, f32[32]{0:T(128)S(1)} %exponential_bitcast_fusion.3), kind=kLoop, calls=%fused_computation.clone.1 | loop fusion | flops 524288 | bytes 3145856 | tf_op jit(solution)/shard_map/while/body/add | solution.py:78
  193.7 3.2 %bitcast_add_fusion.2 = f32[32,128,64]{2,1,0:T(8,128)} fusion(f32[1,32,128,64]{3,2,1,0:T(8,128)S(1)} %copy.97, f32[32,128,64]{2,1,0:T(8,128)} %get-tuple-element.370, f32[32]{0:T(128)S(1)} %exponential_bitcast_fusion.3), kind=kLoop, calls=%fused_computation.clone.1 | loop fusion | flops 524288 | bytes 3145856 | tf_op jit(solution)/shard_map/while/body/add | solution.py:78
  198.8 3.2 %bitcast_add_fusion.2 = f32[32,128,64]{2,1,0:T(8,128)} fusion(f32[1,32,128,64]{3,2,1,0:T(8,128)S(1)} %copy.97, f32[32,128,64]{2,1,0:T(8,128)} %get-tuple-element.370, f32[32]{0:T(128)S(1)} %exponential_bitcast_fusion.3), kind=kLoop, calls=%fused_computation.clone.1 | loop fusion | flops 524288 | bytes 3145856 | tf_op jit(solution)/shard_map/while/body/add | solution.py:78
  203.9 3.2 %bitcast_add_fusion.2 = f32[32,128,64]{2,1,0:T(8,128)} fusion(f32[1,32,128,64]{3,2,1,0:T(8,128)S(1)} %copy.97, f32[32,128,64]{2,1,0:T(8,128)} %get-tuple-element.370, f32[32]{0:T(128)S(1)} %exponential_bitcast_fusion.3), kind=kLoop, calls=%fused_computation.clone.1 | loop fusion | flops 524288 | bytes 3145856 | tf_op jit(solution)/shard_map/while/body/add | solution.py:78
  209.3 2.8 add_convert_fusion
  212.1 4.5 %fusion.17 = f32[4,2,16,64,256]{4,3,2,1,0:T(8,128)} fusion(bf16[4,2,16,128,64]{3,4,2,1,0:T(8,128)(2,1)S(1)} %bitcast.133, bf16[4,256,2,1,128]{4,3,2,1,0:T(2,128)(2,1)S(1)} %copy-done.3), kind=kOutput, calls=%fused_computation.57 | convolution fusion | flops 536870912 | bytes 11010048 | tf_op jit(solution)/shard_map/kign,kgrnp->kigrp/dot_general | solution.py:130
  216.6 12.0 %multiply_add_fusion = f32[4,256,32,64]{1,3,2,0:T(8,128)} fusion(f32[4,256,32,64]{1,3,2,0:T(8,128)} %get-tuple-element.99, f32[4,256,32,64]{1,3,2,0:T(8,128)} %bitcast.130, f32[4,256,32]{1,2,0:T(8,128)S(1)} %exponential_bitcast_fusion.1), kind=kLoop, calls=%fused_computation.40 | loop fusion | flops 4194304 | bytes 25296896 | tf_op jit(solution)/shard_map/add | solution.py:134
  228.6 13.8 %copy.67 = f32[4,256,32,64]{1,0,3,2:T(4,128)} copy(f32[4,256,32,64]{1,3,2,0:T(8,128)} %multiply_add_fusion) | data formatting | bytes 16777216 | tf_op jit(solution)/shard_map/add | solution.py:134
  242.3 5.9 %copy.77 = f32[256,8,4,256]{3,1,2,0:T(8,128)S(1)} copy(f32[256,8,4,256]{3,2,1,0:T(4,128)} %bitcast.132) | data formatting | bytes 16777216
  248.3 6.0 %multiply_reduce_fusion = (f32[1024]{0:T(1024)S(1)}, f32[1024,2048]{0,1:T(8,128)}) fusion(bf16[1024,2048]{0,1:T(8,128)(2,1)S(1)} %copy-done.2, f32[1024,2048]{0,1:T(8,128)S(1)} %bitcast.131, bf16[1024,2048]{0,1:T(8,128)(2,1)S(1)} %copy-done.1, f32[2048]{0:T(1024)S(1)} %mul.285), kind=kLoop, calls=%fused_computation.39 | loop fusion | flops 23067648 | bytes 25178112 | tf_op jit(solution)/shard_map/reduce_sum | solution.py:138
  254.2 9.6 %psum.7 = f32[1024]{0:T(1024)S(1)} all-reduce(f32[1024]{0:T(1024)S(1)} %get-tuple-element.220), channel_id=1, replica_groups=mesh['seq'=8,'tp'=4] {'tp'}, use_global_device_ids=true, to_apply=%region_9.10 | all-reduce | flops 1024 | bytes 8192 | tf_op jit(solution)/shard_map/psum | solution.py:139
  263.9 5.2 %multiply_convert_fusion = bf16[1024,2048]{0,1:T(8,128)(2,1)} fusion(f32[1024,2048]{0,1:T(8,128)} %get-tuple-element.221, f32[2048]{0:T(1024)S(1)} %copy-done.7, f32[1024]{0:T(1024)S(1)} %add_rsqrt_fusion), kind=kLoop, calls=%fused_computation.38 | loop fusion | flops 6291456 | bytes 12595200 | tf_op jit(solution)/shard_map/convert_element_type | solution.py:141
  269.1 6.4 %copy.69 = bf16[1024,2048]{1,0:T(8,128)(2,1)} copy(bf16[1024,2048]{0,1:T(8,128)(2,1)} %multiply_convert_fusion) | data formatting | bytes 8388608 | tf_op jit(solution)/shard_map/convert_element_type | solution.py:141
  (171 shorter events, 66.2 us)
Async XLA Ops:
  6.5 163.2 %all-gather.4.cloned.1.call-start = ((), (), s32[]{:S(2)}) async-start(), calls=%async_computation | async-start | bytes 9437184 | tf_op jit(solution)/shard_map/all_gather | solution.py:23
  8.4 16.0 %collective-permute-start.1 = (bf16[3,2048]{0,1:T(8,128)(2,1)}, bf16[3,2048]{0,1:T(8,128)(2,1)}, u32[]{:S(2)}, u32[]{:S(2)}) collective-permute-start(bf16[3,2048]{0,1:T(8,128)(2,1)} %copy.57), channel_id=1, source_target_pairs={{0,4},{4,8},{8,12},{12,16},{16,20},{20,24},{24,28},{1,5},{5,9},{9,... | collective-permute-start | bytes 36872 | tf_op jit(solution)/shard_map/ppermute | solution.py:18
  10.4 11.4 %collective-permute-start = (bf16[3,512]{1,0:T(4,128)(2,1)S(1)}, bf16[3,512]{1,0:T(4,128)(2,1)S(1)}, u32[]{:S(2)}, u32[]{:S(2)}) collective-permute-start(bf16[3,512]{1,0:T(4,128)(2,1)S(1)} %slice.70), channel_id=1, source_target_pairs={{0,4},{4,8},{8,12},{12,16},{16,20},{20,24},{24,28},{1,5},{5,9},{9,... | collective-permute-start | bytes 9224 | tf_op jit(solution)/shard_map/ppermute | solution.py:18
  15.1 6.7 %copy-start.4 = (bf16[1024,512]{1,0:T(8,128)(2,1)S(1)}, bf16[1024,512]{1,0:T(8,128)(2,1)}, u32[]{:S(2)}) copy-start(bf16[1024,512]{1,0:T(8,128)(2,1)} %param.17) | copy-start | bytes 3145732
  15.1 6.7 %copy-start.8 = (f32[512]{0:T(512)S(1)}, f32[512]{0:T(512)}, u32[]{:S(2)}) copy-start(f32[512]{0:T(512)} %param.23) | copy-start | bytes 6148
  21.6 2.8 %copy-start.6 = (f32[2048]{0:T(1024)S(1)}, f32[2048]{0:T(1024)}, u32[]{:S(2)}) copy-start(f32[2048]{0:T(1024)} %param.22) | copy-start | bytes 24580
  111.5 1.0 copy-start
  112.6 6.5 %copy-start.9 = (f32[32]{0:T(128)S(1)}, f32[32]{0:T(128)}, u32[]{:S(2)}) copy-start(f32[32]{0:T(128)} %param.26) | copy-start | bytes 388
  112.6 6.6 %copy-start.10 = (u32[32]{0:T(128)S(1)}, u32[32]{0:T(128)}, u32[]{:S(2)}) copy-start(u32[32]{0:T(128)} %constant.72) | copy-start | bytes 388
  112.6 11.2 %copy-start.5 = (f32[4,32,256]{2,1,0:T(8,128)S(1)}, f32[4,32,256]{2,1,0:T(8,128)}, u32[]{:S(2)}) copy-start(f32[4,32,256]{2,1,0:T(8,128)} %get-tuple-element.100) | copy-start | bytes 393220
  209.3 2.8 %copy-start.3 = (bf16[4,256,2,1,128]{4,3,2,1,0:T(2,128)(2,1)S(1)}, bf16[4,256,2,1,128]{4,3,2,1,0:T(2,128)(2,1)}, u32[]{:S(2)}) copy-start(bf16[4,256,2,1,128]{4,3,2,1,0:T(2,128)(2,1)} %slice.105) | copy-start | bytes 1572868
  242.3 5.9 %copy-start.1 = (bf16[1024,2048]{0,1:T(8,128)(2,1)S(1)}, bf16[1024,2048]{0,1:T(8,128)(2,1)}, u32[]{:S(2)}) copy-start(bf16[1024,2048]{0,1:T(8,128)(2,1)} %multiply_convert_fusion.1) | copy-start | bytes 12582916
  242.3 5.9 %copy-start.2 = (bf16[1024,2048]{0,1:T(8,128)(2,1)S(1)}, bf16[1024,2048]{0,1:T(8,128)(2,1)}, u32[]{:S(2)}) copy-start(bf16[1024,2048]{0,1:T(8,128)(2,1)} %copy.68) | copy-start | bytes 12582916
  248.3 15.6 %copy-start.7 = (f32[2048]{0:T(1024)S(1)}, f32[2048]{0:T(1024)}, u32[]{:S(2)}) copy-start(f32[2048]{0:T(1024)} %param.27) | copy-start | bytes 24580
Sparse Core Ops, SparseCore 0:
  112.7 56.9 all-gather.3
where the time goes:
time: 284 us; the launch traced here: 282 us
  other arithmetic  94.2 us (33%)
  local copies, waits for them, and re-layouts  87.2 us (31%)
  waiting for transfers between devices  32.2 us (11%)
  matrix products  28.6 us (10%)
  blocking collectives  22.7 us (8%)
  between operations  14.2 us (5%)
    all_gather x1, waiting for transfers between devices, prefix(): gathered = jax.tree.map(lambda a: lax.all_gather(a, axis), part)  32.2 us
    unnamed x29, local copies, waits for them, and re-layouts  25.7 us
    add x7, other arithmetic, join(): jnp.exp(later[0])[:, None, None] * earlier[1] + later[1]  22.3 us
    convert_element_type x2, other arithmetic, causal_conv(): return jax.nn.silu(total).astype(jnp.bfloat16)  19.6 us
    dot_general x4, matrix products, span_local(): jnp.einsum('hij,jhp->ihp', mixing, x_block, preferred_element_type=jnp.fl...  15.8 us
    add x1, local copies, waits for them, and re-layouts, local(): y_intra + y_state  13.8 us
    dynamic_slice x14, local copies, waits for them, and re-layouts, one(): lax.dynamic_index_in_dim(a, turn, 0, False)  13.3 us
    unnamed x1, blocking collectives  13 us
  transfers between devices with their start and end apart: 3, of which 1 were waited for; matrix products, arithmetic and copies ran while one was open for 9% of the time, Pallas kernels for 0%

commit v1 on v0

v1 whole, which is shorter than its diff:
```python
import functools

import jax
import jax.numpy as jnp
from jax import lax
from jax.experimental import pallas as pl
from jax.experimental.pallas import tpu as pltpu
from jax.sharding import PartitionSpec as P

HEAD_DIM = 64
STATE = 128
SPAN = 256
LANES = 256
PIECE = 64
RIM = 16
DECAY_ROWS = 16

epsilon = 1e-05

F32 = jnp.float32
BF16 = jnp.bfloat16
MESH = pl.DeviceIdType.MESH


def silu(value):
    half = 0.5 * value
    return half + half * jnp.tanh(half)


def conv_piece(buffer, row, lanes, taps):
    raw = buffer[pl.ds(row, PIECE + RIM), lanes].astype(F32)
    total = raw[RIM - 3 : RIM - 3 + PIECE] * taps[0:1, lanes] + taps[4:5, lanes]
    for k in range(1, 4):
        total = total + raw[RIM - 3 + k : RIM - 3 + k + PIECE] * taps[k : k + 1, lanes]
    return silu(total).astype(BF16)


def two_rows(row):
    high = row.astype(BF16).astype(F32)
    low = row - high
    width = row.shape[1]
    return jnp.concatenate(
        [jnp.broadcast_to(high, (8, width)), jnp.broadcast_to(low, (8, width))], 0
    ).astype(BF16)


def read_row(pair):
    wide = pair.astype(F32)
    return wide[0:1] + wide[8:9]


def scan_kernel(
    n_seq,
    n_tp,
    steps,
    x_hbm,
    bc_hbm,
    z_hbm,
    dt_ref,
    taps_x,
    taps_bc,
    head_ref,
    gated_hbm,
    total_ref,
    xb,
    bcb,
    zb,
    xc,
    xp,
    bcc,
    tt,
    rn,
    rp,
    dec,
    pre,
    u,
    ls,
    own,
    p_buf,
    q_buf,
    gb,
    sm,
    skip_row,
    sq,
    i_buf,
    e_buf,
    d_buf,
    sa,
    ra,
    sk,
    rk,
    se,
    re,
    ss,
    rs,
    in_sem,
    out_sem,
    send_sem,
    recv_sem,
):
    tokens, width = x_hbm.shape
    heads = dt_ref.shape[0]
    groups = bc_hbm.shape[1] // (2 * STATE)
    group_width = width // groups
    half_width = width // 2
    blocks = tokens // SPAN
    chunks = width // LANES
    half_chunks = half_width // LANES
    seq = lax.axis_index("seq")
    tp = lax.axis_index("tp")
    chip, core = seq // 2, seq % 2
    partner = seq + 1 - 2 * core
    chips = n_seq // 2

    def rows_of(b):
        return pl.ds(b * SPAN, SPAN)

    loads = []
    for b in range(blocks):
        loads.append(
            (
                pltpu.make_async_copy(
                    bc_hbm.at[rows_of(b), :],
                    bcb.at[pl.ds(RIM + b * SPAN, SPAN), :],
                    in_sem.at[0, b],
                ),
                pltpu.make_async_copy(
                    x_hbm.at[rows_of(b), :],
                    xb.at[pl.ds(RIM + b * SPAN, SPAN), :],
                    in_sem.at[1, b],
                ),
                pltpu.make_async_copy(z_hbm.at[rows_of(b), :], zb.at[rows_of(b), :], in_sem.at[2, b]),
            )
        )
    for b in range(blocks):
        loads[b][0].start()
        loads[b][1].start()
    for b in range(blocks):
        loads[b][2].start()

    def at_seq(place):
        return {"seq": place, "tp": tp}

    barrier = pltpu.get_barrier_semaphore()
    sources = [at_seq((seq + n_seq - 1) % n_seq), at_seq(partner)]
    for j in range(steps):
        sources.append(at_seq(((chip + chips - 2**j) % chips) * 2 + core))
    for k in range(1, n_tp):
        sources.append({"seq": seq, "tp": (tp + n_tp - k) % n_tp})
    for source in sources:
        pl.semaphore_signal(barrier, inc=1, device_id=source, device_id_type=MESH)
    pl.semaphore_wait(barrier, len(sources))

    def remote(source, target, slot, device):
        return pltpu.make_async_remote_copy(
            src_ref=source,
            dst_ref=target,
            send_sem=send_sem.at[slot],
            recv_sem=recv_sem.at[slot],
            device_id=device,
            device_id_type=MESH,
        )

    following = at_seq((seq + 1) % n_seq)
    last_rows = pl.ds(tokens - RIM, RIM)
    rim_x = remote(x_hbm.at[last_rows, :], xb.at[pl.ds(0, RIM), :], 0, following)
    rim_bc = remote(bc_hbm.at[last_rows, :], bcb.at[pl.ds(0, RIM), :], 1, following)
    rim_x.start()
    rim_bc.start()

    row_id = lax.broadcasted_iota(jnp.int32, (256, LANES), 0) % 128
    lane_id = lax.broadcasted_iota(jnp.int32, (256, LANES), 1) // HEAD_DIM
    for c in range(chunks):
        lanes = pl.ds(c * LANES, LANES)
        head = lane_id + c * (LANES // HEAD_DIM)
        rn[:, lanes] = jnp.where(row_id == head, 1.0, 0.0).astype(BF16)
        rp[:, lanes] = jnp.where(row_id == head + heads, 1.0, 0.0).astype(BF16)
    upper = jnp.where(
        lax.broadcasted_iota(jnp.int32, (SPAN, SPAN), 0)
        <= lax.broadcasted_iota(jnp.int32, (SPAN, SPAN), 1),
        1.0,
        0.0,
    )
    rate = -jnp.exp(head_ref[:, 1:2])
    for b in range(blocks):
        raw = dt_ref[:, rows_of(b)].astype(F32) + head_ref[:, 0:1]
        step = jnp.maximum(raw, 0.0) + jnp.log(1.0 + jnp.exp(-jnp.abs(raw)))
        cum = jnp.dot(
            rate * step, upper, precision=lax.Precision.HIGHEST, preferred_element_type=F32
        )
        parts = [jnp.exp(-cum) * step, jnp.exp(cum)]
        if 2 * heads < 128:
            parts.append(jnp.zeros((128 - 2 * heads, SPAN), F32))
        turned = jnp.concatenate(parts, 0).T
        high = turned.astype(BF16)
        tt[rows_of(b), 0:128] = high
        tt[rows_of(b), 128:256] = (turned - high.astype(F32)).astype(BF16)
    skip_wide = jnp.broadcast_to(head_ref[:, 2:3], (heads, 128)).T[0:16]
    skip_high = skip_wide.astype(BF16)
    skip_low = (skip_wide - skip_high.astype(F32)).astype(BF16)
    for c in range(chunks):
        lanes = pl.ds(c * LANES, LANES)
        skip_row[:, lanes] = (
            jnp.dot(skip_high, rn[0:heads, lanes], preferred_element_type=F32)
            + jnp.dot(skip_low, rn[0:heads, lanes], preferred_element_type=F32)
        )[0:8]
        running = jnp.ones((1, LANES), F32)
        for b in range(blocks):
            ends = jnp.dot(
                tt[pl.ds((b + 1) * SPAN - 16, 16), :], rp[:, lanes], preferred_element_type=F32
            )
            dec[b : b + 1, lanes] = ends[15:16]
            pre[b : b + 1, lanes] = running
            running = running * ends[15:16]
        pre[blocks : blocks + 1, lanes] = running

    def conv_block(b):
        def bc_piece(r, carry):
            row = pl.multiple_of(b * SPAN + r * PIECE, PIECE)
            for c in range(2 * groups * STATE // LANES):
                lanes = pl.ds(c * LANES, LANES)
                bcc[pl.ds(row, PIECE), lanes] = conv_piece(bcb, row, lanes, taps_bc)
            return carry

        lax.fori_loop(0, SPAN // PIECE, bc_piece, 0)

        def x_chunk(c, carry):
            lanes = pl.ds(pl.multiple_of(c * LANES, LANES), LANES)
            scale = jnp.dot(tt[rows_of(b), :], rn[:, lanes], preferred_element_type=F32)
            for r in range(SPAN // PIECE):
                row = b * SPAN + r * PIECE
                conv = conv_piece(xb, row, lanes, taps_x)
                xc[pl.ds(row, PIECE), lanes] = conv
                xp[pl.ds(row, PIECE), lanes] = (
                    conv.astype(F32) * scale[r * PIECE : (r + 1) * PIECE]
                ).astype(BF16)
            group = c // (group_width // LANES)
            b_part = bcc[rows_of(b), pl.ds(pl.multiple_of(group * 2 * STATE, STATE), STATE)]
            u[b, :, lanes] = lax.dot_general(
                b_part, xp[rows_of(b), lanes], (((0,), (0,)), ((), ())), preferred_element_type=F32
            )
            return carry

        lax.fori_loop(0, chunks, x_chunk, 0)

    loads[0][0].wait()
    loads[0][1].wait()
    for b in range(1, blocks):
        loads[b][0].wait()
        loads[b][1].wait()
        conv_block(b)
    rim_x.wait()
    rim_bc.wait()
    inner = (seq > 0).astype(F32)
    xb[0:RIM, :] = (xb[0:RIM, :].astype(F32) * inner).astype(BF16)
    bcb[0:RIM, :] = (bcb[0:RIM, :].astype(F32) * inner).astype(BF16)
    conv_block(0)

    def carry_chunk(c, carry):
        lanes = pl.ds(pl.multiple_of(c * LANES, LANES), LANES)
        half = c // half_chunks
        local = pl.ds(pl.multiple_of((c % half_chunks) * LANES, LANES), LANES)
        state = jnp.zeros((STATE, LANES), F32)
        for b in range(blocks):
            ls[b, :, lanes] = state.astype(BF16)
            state = dec[b : b + 1, lanes] * (state + u[b, :, lanes])
        own[:, lanes] = state
        sa[half, 0:STATE, local] = state.astype(BF16)
        sa[half, STATE : STATE + DECAY_ROWS, local] = two_rows(pre[blocks : blocks + 1, lanes])
        return carry

    lax.fori_loop(0, chunks, carry_chunk, 0)
    pair = remote(sa, ra, 2, at_seq(partner))
    pair.start()

    causal = lax.broadcasted_iota(jnp.int32, (SPAN, SPAN), 0) >= lax.broadcasted_iota(
        jnp.int32, (SPAN, SPAN), 1
    )

    def intra_block(b):
        loads[b][2].wait()
        for g in range(groups):
            b_part = bcc[rows_of(b), pl.ds(g * 2 * STATE, STATE)]
            c_part = bcc[rows_of(b), pl.ds(g * 2 * STATE + STATE, STATE)]
            scores = lax.dot_general(
                c_part, b_part, (((1,), (1,)), ((), ())), preferred_element_type=F32
            )
            sm[g] = jnp.where(causal, scores, 0.0).astype(BF16)

        def chunk(c, carry):
            lanes = pl.ds(pl.multiple_of(c * LANES, LANES), LANES)
            group = c // (group_width // LANES)
            c_part = bcc[
                rows_of(b), pl.ds(pl.multiple_of(group * 2 * STATE + STATE, STATE), STATE)
            ]
            y = jnp.dot(sm[group], xp[rows_of(b), lanes], preferred_element_type=F32)
            y = y + jnp.dot(c_part, ls[b, :, lanes], preferred_element_type=F32)
            scale = jnp.dot(tt[rows_of(b), :], rp[:, lanes], preferred_element_type=F32)
            for r in range(SPAN // PIECE):
                part = slice(r * PIECE, (r + 1) * PIECE)
                rows = pl.ds(b * SPAN + r * PIECE, PIECE)
                gate = silu(zb[rows, lanes].astype(F32))
                mixed = scale[part] * y[part] + skip_row[0:1, lanes] * xc[rows, lanes].astype(F32)
                p_buf[rows, lanes] = mixed * gate
                q_buf[rows, lanes] = scale[part] * gate
            return carry

        lax.fori_loop(0, chunks, chunk, 0)

    flag = core.astype(F32)

    def joined_chunk(j, carry):
        local = pl.ds(pl.multiple_of(j * LANES, LANES), LANES)
        lanes = pl.ds(pl.multiple_of(core * half_width + j * LANES, LANES), LANES)
        mine, mine_decay = own[:, lanes], pre[blocks : blocks + 1, lanes]
        other = ra[core, 0:STATE, local].astype(F32)
        other_decay = read_row(ra[core, STATE : STATE + DECAY_ROWS, local])
        joined = (1.0 - flag) * (other_decay * mine + other) + flag * (mine_decay * other + mine)
        decay = mine_decay * other_decay
        i_buf[:, local] = joined
        e_buf[:, local] = jnp.zeros_like(joined)
        d_buf[0:1, local] = decay
        d_buf[1:2, local] = jnp.ones_like(decay)
        sk[0, 0:STATE, local] = joined.astype(BF16)
        sk[0, STATE : STATE + DECAY_ROWS, local] = two_rows(decay)
        return carry

    def double(step):
        valid = (chip >= 2**step).astype(F32)

        def body(j, carry):
            local = pl.ds(pl.multiple_of(j * LANES, LANES), LANES)
            got = rk[step, 0:STATE, local].astype(F32) * valid
            got_decay = (
                read_row(rk[step, STATE : STATE + DECAY_ROWS, local]) * valid + (1.0 - valid)
            )
            e_decay = d_buf[1:2, local]
            earlier = e_decay * got + e_buf[:, local]
            e_buf[:, local] = earlier
            d_buf[1:2, local] = e_decay * got_decay
            if step < steps - 1:
                i_decay = d_buf[0:1, local]
                joined = i_decay * got + i_buf[:, local]
                decay = i_decay * got_decay
                i_buf[:, local] = joined
                d_buf[0:1, local] = decay
                sk[step + 1, 0:STATE, local] = joined.astype(BF16)
                sk[step + 1, STATE : STATE + DECAY_ROWS, local] = two_rows(decay)
            else:
                se[:, local] = earlier.astype(BF16)
            return carry

        lax.fori_loop(0, half_chunks, body, 0)

    def hop(step):
        target = at_seq(((chip + 2**step) % chips) * 2 + core)
        return remote(sk.at[step], rk.at[step], 4 + step, target)

    done = 0
    intra_block(done)
    done += 1
    pair.wait()
    lax.fori_loop(0, half_chunks, joined_chunk, 0)
    for step in range(steps):
        moving = hop(step)
        moving.start()
        if done < blocks:
            intra_block(done)
            done += 1
        moving.wait()
        double(step)
    back = remote(se, re, 3, at_seq(partner))
    back.start()
    while done < blocks:
        intra_block(done)
        done += 1
    back.wait()

    def incoming_chunk(c, carry):
        lanes = pl.ds(pl.multiple_of(c * LANES, LANES), LANES)
        half = c // half_chunks
        local = pl.ds(pl.multiple_of((c % half_chunks) * LANES, LANES), LANES)
        here = (half == core).astype(F32)
        state = here * e_buf[:, local] + (1.0 - here) * re[:, local].astype(F32)
        other = ra[half, 0:STATE, local].astype(F32)
        other_decay = read_row(ra[half, STATE : STATE + DECAY_ROWS, local])
        own[:, lanes] = (1.0 - flag) * state + flag * (other_decay * state + other)
        return carry

    lax.fori_loop(0, chunks, incoming_chunk, 0)

    stores = []
    for b in range(blocks):
        sq[...] = jnp.zeros_like(sq)

        def final(c, carry):
            lanes = pl.ds(pl.multiple_of(c * LANES, LANES), LANES)
            group = c // (group_width // LANES)
            c_part = bcc[
                rows_of(b), pl.ds(pl.multiple_of(group * 2 * STATE + STATE, STATE), STATE)
            ]
            start = (own[:, lanes] * pre[b : b + 1, lanes]).astype(BF16)
            y = jnp.dot(c_part, start, preferred_element_type=F32)
            for r in range(SPAN // PIECE):
                part = slice(r * PIECE, (r + 1) * PIECE)
                rows = pl.ds(b * SPAN + r * PIECE, PIECE)
                gated = p_buf[rows, lanes] + q_buf[rows, lanes] * y[part]
                gb[rows, lanes] = gated.astype(BF16)
                square = gated * gated
                total = square[:, 0:128]
                for i in range(1, LANES // 128):
                    total = total + square[:, i * 128 : (i + 1) * 128]
                sq[pl.ds(r * PIECE, PIECE), :] += total
            return carry

        lax.fori_loop(0, chunks, final, 0)
        ss[:, pl.ds(b * SPAN, SPAN)] = jnp.broadcast_to(
            jnp.sum(sq[...].T, axis=0, keepdims=True), (8, SPAN)
        )
        store = pltpu.make_async_copy(gb.at[rows_of(b), :], gated_hbm.at[rows_of(b), :], out_sem.at[b])
        store.start()
        stores.append(store)

    shares = []
    for k in range(1, n_tp):
        share = remote(
            ss, rs.at[k - 1], 3 + steps + k, {"seq": seq, "tp": (tp + k) % n_tp}
        )
        share.start()
        shares.append(share)
    for share in shares:
        share.wait()
    total = ss[...]
    for k in range(n_tp - 1):
        total = total + rs[k]
    total_ref[...] = lax.rsqrt(total * (1.0 / (width * n_tp)) + epsilon)
    for store in stores:
        store.wait()


def scale_kernel(gated_ref, factor_ref, gain_ref, out_ref):
    column = factor_ref[...].T[:, 0:1]
    for r in range(0, gated_ref.shape[0], PIECE):
        rows = pl.ds(r, PIECE)
        wide = gated_ref[rows, :].astype(F32)
        out_ref[rows, :] = (wide * column[r : r + PIECE] * gain_ref[...]).astype(BF16)


def local(
    n_seq,
    n_tp,
    x_input,
    bc_input,
    z_gate,
    dt_input,
    conv_weight_x,
    conv_weight_bc,
    conv_bias_x,
    conv_bias_bc,
    dt_bias,
    decay_log,
    skip_scale,
    norm_gain,
):
    tokens, width = x_input.shape
    bc_width = bc_input.shape[1]
    heads = dt_input.shape[0]
    groups = bc_width // (2 * STATE)
    blocks = tokens // SPAN
    half_width = width // 2
    steps = max(1, (n_seq // 2 - 1).bit_length())

    def taps(weight, bias):
        return jnp.concatenate(
            [weight.astype(F32), bias[None, :], jnp.zeros((3, bias.shape[0]), F32)], 0
        )

    none = jnp.zeros_like(dt_bias)
    head_rows = jnp.stack([dt_bias, decay_log, skip_scale, none, none, none, none, none], axis=1)
    whole = pl.BlockSpec(memory_space=pltpu.VMEM)
    anywhere = pl.BlockSpec(memory_space=pl.ANY)
    message = STATE + DECAY_ROWS
    copies = 4 + steps + n_tp - 1
    gated, factor = pl.pallas_call(
        functools.partial(scan_kernel, n_seq, n_tp, steps),
        out_shape=(
            jax.ShapeDtypeStruct((tokens, width), BF16),
            jax.ShapeDtypeStruct((8, tokens), F32),
        ),
        in_specs=[anywhere] * 3 + [whole] * 4,
        out_specs=(anywhere, whole),
        scratch_shapes=[
            pltpu.VMEM((RIM + tokens, width), BF16),
            pltpu.VMEM((RIM + tokens, bc_width), BF16),
            pltpu.VMEM((tokens, width), BF16),
            pltpu.VMEM((tokens, width), BF16),
            pltpu.VMEM((tokens, width), BF16),
            pltpu.VMEM((tokens, bc_width), BF16),
            pltpu.VMEM((tokens, 256), BF16),
            pltpu.VMEM((256, width), BF16),
            pltpu.VMEM((256, width), BF16),
            pltpu.VMEM((8, width), F32),
            pltpu.VMEM((8, width), F32),
            pltpu.VMEM((blocks, STATE, width), F32),
            pltpu.VMEM((blocks, STATE, width), BF16),
            pltpu.VMEM((STATE, width), F32),
            pltpu.VMEM((tokens, width), F32),
            pltpu.VMEM((tokens, width), F32),
            pltpu.VMEM((tokens, width), BF16),
            pltpu.VMEM((groups, SPAN, SPAN), BF16),
            pltpu.VMEM((8, width), F32),
            pltpu.VMEM((SPAN, 128), F32),
            pltpu.VMEM((STATE, half_width), F32),
            pltpu.VMEM((STATE, half_width), F32),
            pltpu.VMEM((8, half_width), F32),
            pltpu.VMEM((2, message, half_width), BF16),
            pltpu.VMEM((2, message, half_width), BF16),
            pltpu.VMEM((steps, message, half_width), BF16),
            pltpu.VMEM((steps, message, half_width), BF16),
            pltpu.VMEM((STATE, half_width), BF16),
            pltpu.VMEM((STATE, half_width), BF16),
            pltpu.VMEM((8, tokens), F32),
            pltpu.VMEM((n_tp - 1, 8, tokens), F32),
            pltpu.SemaphoreType.DMA((3, blocks)),
            pltpu.SemaphoreType.DMA((blocks,)),
            pltpu.SemaphoreType.DMA((copies,)),
            pltpu.SemaphoreType.DMA((copies,)),
        ],
        compiler_params=pltpu.CompilerParams(
            collective_id=0, has_side_effects=True, vmem_limit_bytes=60 * 1024 * 1024
        ),
        name="scan",
    )(
        x_input,
        bc_input,
        z_gate,
        dt_input,
        taps(conv_weight_x, conv_bias_x),
        taps(conv_weight_bc, conv_bias_bc),
        head_rows,
    )
    return pl.pallas_call(
        scale_kernel,
        grid=(blocks,),
        out_shape=jax.ShapeDtypeStruct((tokens, width), BF16),
        in_specs=[
            pl.BlockSpec((SPAN, width), lambda i: (i, 0)),
            pl.BlockSpec((8, SPAN), lambda i: (0, i)),
            pl.BlockSpec((1, width), lambda i: (0, 0)),
        ],
        out_specs=pl.BlockSpec((SPAN, width), lambda i: (i, 0)),
        name="scale",
    )(gated, factor, norm_gain[None, :])


def solution(mesh):
    in_specs = (
        P("seq", "tp"),
        P("seq", "tp"),
        P("seq", "tp"),
        P("tp", "seq"),
        P(None, "tp"),
        P(None, "tp"),
        P("tp"),
        P("tp"),
        P("tp"),
        P("tp"),
        P("tp"),
        P("tp"),
    )
    body = functools.partial(local, mesh.shape["seq"], mesh.shape["tp"])
    return jax.shard_map(
        body, mesh=mesh, in_specs=in_specs, out_specs=P("seq", "tp"), check_vma=False
    )
```

time: 284 us -> 72.8 us (0.26)
  the two profiles are of different devices: /device:TPU:7 before, /device:TPU:0 now
where the time goes in v1:
time: 72.8 us; the launch traced here: 72.4 us
  Pallas kernels  66.7 us (92%)
  other arithmetic  4.16 us (6%)
  local copies, waits for them, and re-layouts  1.46 us (2%)
    pallas_call x1, Pallas kernels, local(): pl.pallas_call(functools.partial(scan_kernel, n_seq, n_tp, steps), out_sh...  61.2 us
    pallas_call x1, Pallas kernels, local(): pl.pallas_call(scale_kernel, grid=(blocks,), out_shape=jax.ShapeDtypeStru...  5.49 us
    concatenate x2, other arithmetic, taps(): jnp.concatenate([weight.astype(F32), bias[None, :], jnp.zeros((3, bias.sh...  2.75 us

profile of v1, /device:TPU:0, one launch (start us, length us, event | category | flops | bytes accessed | tf_op | source)
XLA Modules:
  0.0 72.4 jit_solution(9052511282643423590)
XLA Ops:
  0.0 0.1 pad.5.clone
  0.1 0.7 stack.19
  0.8 0.7 convert_element_type.7
  1.5 1.3 %maximum_maximum_fusion.1.taps_bc = f32[8,512]{1,0:T(8,128)} fusion(f32[1,512]{1,0:T(1,128)} %bitcast.8, f32[4,512]{1,0:T(4,128)S(1)} %convert_element_type.7, f32[8]{0:T(128)S(1)} %pad.5.clone), kind=kLoop, calls=%fused_computation.1 | loop fusion | flops 8192 | bytes 26656 | tf_op jit(solution)/shard_map/concatenate | solution.py:474
  2.8 0.7 copy.16.head_ref
  3.5 0.7 convert_element_type.6
  4.2 1.4 %maximum_maximum_fusion.taps_x = f32[8,2048]{1,0:T(8,128)} fusion(f32[1,2048]{1,0:T(1,128)} %bitcast.7, f32[4,2048]{1,0:T(4,128)S(1)} %convert_element_type.6, f32[8]{0:T(128)S(1)} %pad.5.clone), kind=kLoop, calls=%fused_computation | loop fusion | flops 32768 | bytes 106528 | tf_op jit(solution)/shard_map/concatenate | solution.py:474
  5.6 61.2 %scan.1 = (bf16[1024,2048]{1,0:T(8,128)(2,1)}, f32[8,1024]{1,0:T(8,128)}) custom-call(bf16[1024,2048]{1,0:T(8,128)(2,1)} %x_hbm.1, bf16[1024,512]{1,0:T(8,128)(2,1)} %bc_hbm.1, bf16[1024,2048]{1,0:T(8,128)(2,1)} %z_hbm.1, bf16[32,1024]{1,0:T(8,128)(2,1)} %dt_ref.1, f32[8,2048]{1,0:T(8,128)} %maximum_maximum_fusion.taps_x, ...), custom_call_target="tpu_custom_call" | custom-call | tf_op jit(solution)/shard_map/scan/pallas_call | solution.py:484
  66.9 5.5 %scale.1 = bf16[1024,2048]{1,0:T(8,128)(2,1)} custom-call(bf16[1024,2048]{1,0:T(8,128)(2,1)} %get-tuple-element.7.gated_ref, f32[8,1024]{1,0:T(8,128)} %get-tuple-element.8.factor_ref, f32[1,2048]{1,0:T(1,128)} %bitcast.6), custom_call_target="tpu_custom_call" | custom-call | tf_op jit(solution)/shard_map/scale/pallas_call | solution.py:542
  (3 shorter events, 0.0 us)

commit v2 on v1

--- a/solution.py
+++ b/solution.py
@@ -57,9 +57,13 @@
     bc_hbm,
     z_hbm,
     dt_ref,
-    taps_x,
-    taps_bc,
-    head_ref,
+    weight_x,
+    weight_bc,
+    bias_x,
+    bias_bc,
+    dt_bias,
+    decay_log,
+    skip_scale,
     gated_hbm,
     total_ref,
     xb,
@@ -93,6 +97,8 @@
     re,
     ss,
     rs,
+    taps_x,
+    taps_bc,
     in_sem,
     out_sem,
     send_sem,
@@ -105,7 +111,8 @@
     half_width = width // 2
     blocks = tokens // SPAN
     chunks = width // LANES
-    half_chunks = half_width // LANES
+    quarter = half_width // 2
+    quarter_chunks = quarter // LANES
     seq = lax.axis_index("seq")
     tp = lax.axis_index("tp")
     chip, core = seq // 2, seq % 2
@@ -181,9 +188,20 @@
         1.0,
         0.0,
     )
-    rate = -jnp.exp(head_ref[:, 1:2])
+    eye = lax.broadcasted_iota(jnp.int32, (heads, heads), 0) == lax.broadcasted_iota(
+        jnp.int32, (heads, heads), 1
+    )
+
+    def column(row_ref):
+        return jnp.sum(jnp.where(eye, row_ref[...], 0.0), axis=1, keepdims=True)
+
+    for target, weight, bias in ((taps_x, weight_x, bias_x), (taps_bc, weight_bc, bias_bc)):
+        target[0:4, :] = weight[...].astype(F32)
+        target[4:5, :] = bias[...]
+    rate = -jnp.exp(column(decay_log))
+    shift = column(dt_bias)
     for b in range(blocks):
-        raw = dt_ref[:, rows_of(b)].astype(F32) + head_ref[:, 0:1]
+        raw = dt_ref[:, rows_of(b)].astype(F32) + shift
         step = jnp.maximum(raw, 0.0) + jnp.log(1.0 + jnp.exp(-jnp.abs(raw)))
         cum = jnp.dot(
             rate * step, upper, precision=lax.Precision.HIGHEST, preferred_element_type=F32
@@ -195,7 +213,7 @@
         high = turned.astype(BF16)
         tt[rows_of(b), 0:128] = high
         tt[rows_of(b), 128:256] = (turned - high.astype(F32)).astype(BF16)
-    skip_wide = jnp.broadcast_to(head_ref[:, 2:3], (heads, 128)).T[0:16]
+    skip_wide = jnp.broadcast_to(skip_scale[...], (16, heads))
     skip_high = skip_wide.astype(BF16)
     skip_low = (skip_wide - skip_high.astype(F32)).astype(BF16)
     for c in range(chunks):
@@ -214,7 +232,16 @@
             running = running * ends[15:16]
         pre[blocks : blocks + 1, lanes] = running
 
-    def conv_block(b):
+    def place_of(stage, c):
+        half = c // quarter_chunks
+        inside = stage * quarter + (c % quarter_chunks) * LANES
+        lanes = pl.ds(pl.multiple_of(half * half_width + inside, LANES), LANES)
+        piece = pl.ds(pl.multiple_of((c % quarter_chunks) * LANES, LANES), LANES)
+        local = pl.ds(pl.multiple_of(inside, LANES), LANES)
+        group = (half * half_width + inside) // group_width
+        return half, lanes, piece, local, group
+
+    def conv_block(b, stage):
         def bc_piece(r, carry):
             row = pl.multiple_of(b * SPAN + r * PIECE, PIECE)
             for c in range(2 * groups * STATE // LANES):
@@ -222,10 +249,11 @@
                 bcc[pl.ds(row, PIECE), lanes] = conv_piece(bcb, row, lanes, taps_bc)
             return carry
 
-        lax.fori_loop(0, SPAN // PIECE, bc_piece, 0)
+        if stage == 0:
+            lax.fori_loop(0, SPAN // PIECE, bc_piece, 0)
 
         def x_chunk(c, carry):
-            lanes = pl.ds(pl.multiple_of(c * LANES, LANES), LANES)
+            _, lanes, _, _, group = place_of(stage, c)
             scale = jnp.dot(tt[rows_of(b), :], rn[:, lanes], preferred_element_type=F32)
             for r in range(SPAN // PIECE):
                 row = b * SPAN + r * PIECE
@@ -234,44 +262,44 @@
                 xp[pl.ds(row, PIECE), lanes] = (
                     conv.astype(F32) * scale[r * PIECE : (r + 1) * PIECE]
                 ).astype(BF16)
-            group = c // (group_width // LANES)
             b_part = bcc[rows_of(b), pl.ds(pl.multiple_of(group * 2 * STATE, STATE), STATE)]
             u[b, :, lanes] = lax.dot_general(
                 b_part, xp[rows_of(b), lanes], (((0,), (0,)), ((), ())), preferred_element_type=F32
             )
             return carry
 
-        lax.fori_loop(0, chunks, x_chunk, 0)
+        lax.fori_loop(0, chunks // 2, x_chunk, 0)
 
     loads[0][0].wait()
     loads[0][1].wait()
     for b in range(1, blocks):
         loads[b][0].wait()
         loads[b][1].wait()
-        conv_block(b)
+        conv_block(b, 0)
     rim_x.wait()
     rim_bc.wait()
     inner = (seq > 0).astype(F32)
     xb[0:RIM, :] = (xb[0:RIM, :].astype(F32) * inner).astype(BF16)
     bcb[0:RIM, :] = (bcb[0:RIM, :].astype(F32) * inner).astype(BF16)
-    conv_block(0)
-
-    def carry_chunk(c, carry):
-        lanes = pl.ds(pl.multiple_of(c * LANES, LANES), LANES)
-        half = c // half_chunks
-        local = pl.ds(pl.multiple_of((c % half_chunks) * LANES, LANES), LANES)
+    conv_block(0, 0)
+
+    def carry_chunk(stage, c, carry):
+        half, lanes, piece, _, _ = place_of(stage, c)
         state = jnp.zeros((STATE, LANES), F32)
         for b in range(blocks):
             ls[b, :, lanes] = state.astype(BF16)
             state = dec[b : b + 1, lanes] * (state + u[b, :, lanes])
         own[:, lanes] = state
-        sa[half, 0:STATE, local] = state.astype(BF16)
-        sa[half, STATE : STATE + DECAY_ROWS, local] = two_rows(pre[blocks : blocks + 1, lanes])
+        sa[stage, half, 0:STATE, piece] = state.astype(BF16)
+        sa[stage, half, STATE : STATE + DECAY_ROWS, piece] = two_rows(pre[blocks : blocks + 1, lanes])
         return carry
 
-    lax.fori_loop(0, chunks, carry_chunk, 0)
-    pair = remote(sa, ra, 2, at_seq(partner))
-    pair.start()
+    def pair(stage):
+        return remote(sa.at[stage], ra.at[stage], 2 + stage, at_seq(partner))
+
+    def send_state(stage):
+        lax.fori_loop(0, chunks // 2, functools.partial(carry_chunk, stage), 0)
+        pair(stage).start()
 
     causal = lax.broadcasted_iota(jnp.int32, (SPAN, SPAN), 0) >= lax.broadcasted_iota(
         jnp.int32, (SPAN, SPAN), 1
@@ -309,30 +337,33 @@
 
     flag = core.astype(F32)
 
-    def joined_chunk(j, carry):
-        local = pl.ds(pl.multiple_of(j * LANES, LANES), LANES)
-        lanes = pl.ds(pl.multiple_of(core * half_width + j * LANES, LANES), LANES)
+    def joined_chunk(stage, j, carry):
+        piece = pl.ds(pl.multiple_of(j * LANES, LANES), LANES)
+        inside = stage * quarter + j * LANES
+        local = pl.ds(pl.multiple_of(inside, LANES), LANES)
+        lanes = pl.ds(pl.multiple_of(core * half_width + inside, LANES), LANES)
         mine, mine_decay = own[:, lanes], pre[blocks : blocks + 1, lanes]
-        other = ra[core, 0:STATE, local].astype(F32)
-        other_decay = read_row(ra[core, STATE : STATE + DECAY_ROWS, local])
+        other = ra[stage, core, 0:STATE, piece].astype(F32)
+        other_decay = read_row(ra[stage, core, STATE : STATE + DECAY_ROWS, piece])
         joined = (1.0 - flag) * (other_decay * mine + other) + flag * (mine_decay * other + mine)
         decay = mine_decay * other_decay
         i_buf[:, local] = joined
         e_buf[:, local] = jnp.zeros_like(joined)
         d_buf[0:1, local] = decay
         d_buf[1:2, local] = jnp.ones_like(decay)
-        sk[0, 0:STATE, local] = joined.astype(BF16)
-        sk[0, STATE : STATE + DECAY_ROWS, local] = two_rows(decay)
+        sk[stage, 0, 0:STATE, piece] = joined.astype(BF16)
+        sk[stage, 0, STATE : STATE + DECAY_ROWS, piece] = two_rows(decay)
         return carry
 
-    def double(step):
+    def double(stage, step):
         valid = (chip >= 2**step).astype(F32)
 
         def body(j, carry):
-            local = pl.ds(pl.multiple_of(j * LANES, LANES), LANES)
-            got = rk[step, 0:STATE, local].astype(F32) * valid
+            piece = pl.ds(pl.multiple_of(j * LANES, LANES), LANES)
+            local = pl.ds(pl.multiple_of(stage * quarter + j * LANES, LANES), LANES)
+            got = rk[stage, step, 0:STATE, piece].astype(F32) * valid
             got_decay = (
-                read_row(rk[step, STATE : STATE + DECAY_ROWS, local]) * valid + (1.0 - valid)
+                read_row(rk[stage, step, STATE : STATE + DECAY_ROWS, piece]) * valid + (1.0 - valid)
             )
             e_decay = d_buf[1:2, local]
             earlier = e_decay * got + e_buf[:, local]
@@ -344,58 +375,52 @@
                 decay = i_decay * got_decay
                 i_buf[:, local] = joined
                 d_buf[0:1, local] = decay
-                sk[step + 1, 0:STATE, local] = joined.astype(BF16)
-                sk[step + 1, STATE : STATE + DECAY_ROWS, local] = two_rows(decay)
+                sk[stage, step + 1, 0:STATE, piece] = joined.astype(BF16)
+                sk[stage, step + 1, STATE : STATE + DECAY_ROWS, piece] = two_rows(decay)
             else:
-                se[:, local] = earlier.astype(BF16)
+                se[stage, :, piece] = earlier.astype(BF16)
             return carry
 
-        lax.fori_loop(0, half_chunks, body, 0)
-
-    def hop(step):
+        lax.fori_loop(0, quarter_chunks, body, 0)
+
+    def hop(stage, step):
         target = at_seq(((chip + 2**step) % chips) * 2 + core)
-        return remote(sk.at[step], rk.at[step], 4 + step, target)
-
-    done = 0
-    intra_block(done)
-    done += 1
-    pair.wait()
-    lax.fori_loop(0, half_chunks, joined_chunk, 0)
-    for step in range(steps):
-        moving = hop(step)
-        moving.start()
-        if done < blocks:
-            intra_block(done)
-            done += 1
-        moving.wait()
-        double(step)
-    back = remote(se, re, 3, at_seq(partner))
-    back.start()
-    while done < blocks:
-        intra_block(done)
-        done += 1
-    back.wait()
-
-    def incoming_chunk(c, carry):
-        lanes = pl.ds(pl.multiple_of(c * LANES, LANES), LANES)
-        half = c // half_chunks
-        local = pl.ds(pl.multiple_of((c % half_chunks) * LANES, LANES), LANES)
+        slot = 6 + stage * steps + step
+        return remote(sk.at[stage, step], rk.at[stage, step], slot, target)
+
+    def back(stage):
+        return remote(se.at[stage], re.at[stage], 4 + stage, at_seq(partner))
+
+    def join_pair(stage):
+        pair(stage).wait()
+        lax.fori_loop(0, quarter_chunks, functools.partial(joined_chunk, stage), 0)
+        hop(stage, 0).start()
+
+    def advance(stage, step):
+        hop(stage, step).wait()
+        double(stage, step)
+        if step < steps - 1:
+            hop(stage, step + 1).start()
+        else:
+            back(stage).start()
+
+    def incoming_chunk(stage, c, carry):
+        half, lanes, piece, local, _ = place_of(stage, c)
         here = (half == core).astype(F32)
-        state = here * e_buf[:, local] + (1.0 - here) * re[:, local].astype(F32)
-        other = ra[half, 0:STATE, local].astype(F32)
-        other_decay = read_row(ra[half, STATE : STATE + DECAY_ROWS, local])
+        state = here * e_buf[:, local] + (1.0 - here) * re[stage, :, piece].astype(F32)
+        other = ra[stage, half, 0:STATE, piece].astype(F32)
+        other_decay = read_row(ra[stage, half, STATE : STATE + DECAY_ROWS, piece])
         own[:, lanes] = (1.0 - flag) * state + flag * (other_decay * state + other)
         return carry
 
-    lax.fori_loop(0, chunks, incoming_chunk, 0)
-
     stores = []
-    for b in range(blocks):
-        sq[...] = jnp.zeros_like(sq)
+
+    def final_block(b, stage):
+        if stage == 0:
+            sq[rows_of(b), :] = jnp.zeros((SPAN, 128), F32)
 
         def final(c, carry):
-            lanes = pl.ds(pl.multiple_of(c * LANES, LANES), LANES)
-            group = c // (group_width // LANES)
+            _, lanes, _, _, group = place_of(stage, c)
             c_part = bcc[
                 rows_of(b), pl.ds(pl.multiple_of(group * 2 * STATE + STATE, STATE), STATE)
             ]
@@ -410,21 +435,51 @@
                 total = square[:, 0:128]
                 for i in range(1, LANES // 128):
                     total = total + square[:, i * 128 : (i + 1) * 128]
-                sq[pl.ds(r * PIECE, PIECE), :] += total
+                sq[rows, :] += total
             return carry
 
-        lax.fori_loop(0, chunks, final, 0)
-        ss[:, pl.ds(b * SPAN, SPAN)] = jnp.broadcast_to(
-            jnp.sum(sq[...].T, axis=0, keepdims=True), (8, SPAN)
-        )
-        store = pltpu.make_async_copy(gb.at[rows_of(b), :], gated_hbm.at[rows_of(b), :], out_sem.at[b])
-        store.start()
-        stores.append(store)
+        lax.fori_loop(0, chunks // 2, final, 0)
+        if stage == 1:
+            ss[:, rows_of(b)] = jnp.broadcast_to(
+                jnp.sum(sq[rows_of(b), :].T, axis=0, keepdims=True), (8, SPAN)
+            )
+            store = pltpu.make_async_copy(
+                gb.at[rows_of(b), :], gated_hbm.at[rows_of(b), :], out_sem.at[b]
+            )
+            store.start()
+            stores.append(store)
+
+    def finish(stage):
+        back(stage).wait()
+        lax.fori_loop(0, chunks // 2, functools.partial(incoming_chunk, stage), 0)
+        for b in range(blocks):
+            final_block(b, stage)
+
+    send_state(0)
+    conv_block(0, 1)
+    join_pair(0)
+    for b in range(1, blocks):
+        conv_block(b, 1)
+    advance(0, 0)
+    send_state(1)
+    intra_block(0)
+    join_pair(1)
+    for b in range(1, blocks):
+        intra_block(b)
+        if b == 1:
+            for step in range(1, steps):
+                advance(0, step)
+        if b == 2:
+            advance(1, 0)
+    finish(0)
+    for step in range(1, steps):
+        advance(1, step)
+    finish(1)
 
     shares = []
     for k in range(1, n_tp):
         share = remote(
-            ss, rs.at[k - 1], 3 + steps + k, {"seq": seq, "tp": (tp + k) % n_tp}
+            ss, rs.at[k - 1], 5 + 2 * steps + k, {"seq": seq, "tp": (tp + k) % n_tp}
         )
         share.start()
         shares.append(share)
@@ -467,27 +522,20 @@
     heads = dt_input.shape[0]
     groups = bc_width // (2 * STATE)
     blocks = tokens // SPAN
-    half_width = width // 2
+    quarter = width // 4
     steps = max(1, (n_seq // 2 - 1).bit_length())
 
-    def taps(weight, bias):
-        return jnp.concatenate(
-            [weight.astype(F32), bias[None, :], jnp.zeros((3, bias.shape[0]), F32)], 0
-        )
-
-    none = jnp.zeros_like(dt_bias)
-    head_rows = jnp.stack([dt_bias, decay_log, skip_scale, none, none, none, none, none], axis=1)
     whole = pl.BlockSpec(memory_space=pltpu.VMEM)
     anywhere = pl.BlockSpec(memory_space=pl.ANY)
     message = STATE + DECAY_ROWS
-    copies = 4 + steps + n_tp - 1
+    copies = 6 + 2 * steps + n_tp - 1
     gated, factor = pl.pallas_call(
         functools.partial(scan_kernel, n_seq, n_tp, steps),
         out_shape=(
             jax.ShapeDtypeStruct((tokens, width), BF16),
             jax.ShapeDtypeStruct((8, tokens), F32),
         ),
-        in_specs=[anywhere] * 3 + [whole] * 4,
+        in_specs=[anywhere] * 3 + [whole] * 8,
         out_specs=(anywhere, whole),
         scratch_shapes=[
             pltpu.VMEM((RIM + tokens, width), BF16),
@@ -509,18 +557,20 @@
             pltpu.VMEM((tokens, width), BF16),
             pltpu.VMEM((groups, SPAN, SPAN), BF16),
             pltpu.VMEM((8, width), F32),
-            pltpu.VMEM((SPAN, 128), F32),
-            pltpu.VMEM((STATE, half_width), F32),
-            pltpu.VMEM((STATE, half_width), F32),
-            pltpu.VMEM((8, half_width), F32),
-            pltpu.VMEM((2, message, half_width), BF16),
-            pltpu.VMEM((2, message, half_width), BF16),
-            pltpu.VMEM((steps, message, half_width), BF16),
-            pltpu.VMEM((steps, message, half_width), BF16),
-            pltpu.VMEM((STATE, half_width), BF16),
-            pltpu.VMEM((STATE, half_width), BF16),
+            pltpu.VMEM((tokens, 128), F32),
+            pltpu.VMEM((STATE, 2 * quarter), F32),
+            pltpu.VMEM((STATE, 2 * quarter), F32),
+            pltpu.VMEM((8, 2 * quarter), F32),
+            pltpu.VMEM((2, 2, message, quarter), BF16),
+            pltpu.VMEM((2, 2, message, quarter), BF16),
+            pltpu.VMEM((2, steps, message, quarter), BF16),
+            pltpu.VMEM((2, steps, message, quarter), BF16),
+            pltpu.VMEM((2, STATE, quarter), BF16),
+            pltpu.VMEM((2, STATE, quarter), BF16),
             pltpu.VMEM((8, tokens), F32),
             pltpu.VMEM((n_tp - 1, 8, tokens), F32),
+            pltpu.VMEM((8, width), F32),
+            pltpu.VMEM((8, bc_width), F32),
             pltpu.SemaphoreType.DMA((3, blocks)),
             pltpu.SemaphoreType.DMA((blocks,)),
             pltpu.SemaphoreType.DMA((copies,)),
@@ -535,9 +585,13 @@
         bc_input,
         z_gate,
         dt_input,
-        taps(conv_weight_x, conv_bias_x),
-        taps(conv_weight_bc, conv_bias_bc),
-        head_rows,
+        conv_weight_x,
+        conv_weight_bc,
+        conv_bias_x[None, :],
+        conv_bias_bc[None, :],
+        dt_bias[None, :],
+        decay_log[None, :],
+        skip_scale[None, :],
     )
     return pl.pallas_call(
         scale_kernel,

time: 72.8 us -> 60.2 us (0.83)
  Pallas kernels: 66.7 us -> 60 us
  other arithmetic: 4.16 us -> 0 us
  local copies, waits for them, and re-layouts: 1.46 us -> 0 us
    pallas_call x1, Pallas kernels: 61.2 us -> 54.5 us  [local(): pl.pallas_call(functools.partial(scan_kernel, n_seq, n_tp, steps), out_sh...]
    concatenate x2 -> x0, other arithmetic: 2.75 us -> none  [taps(): jnp.concatenate([weight.astype(F32), bias[None, :], jnp.zeros((3, bias.sh...]
    convert_element_type x2 -> x0, other arithmetic: 1.41 us -> none  [taps(): weight.astype(F32)]
    another operation x4 -> x0, local copies, waits for them, and re-layouts: 1.38 us -> none  [local(): jnp.stack([dt_bias, decay_log, skip_scale, none, none, none, none, none],...]
where the time goes in v2:
time: 60.2 us; the launch traced here: 60 us
  Pallas kernels  60 us (100%)
    pallas_call x1, Pallas kernels, local(): pl.pallas_call(functools.partial(scan_kernel, n_seq, n_tp, steps), out_sh...  54.5 us
    pallas_call x1, Pallas kernels, local(): pl.pallas_call(scale_kernel, grid=(blocks,), out_shape=jax.ShapeDtypeStru...  5.49 us

profile of v2, /device:TPU:0, one launch (start us, length us, event | category | flops | bytes accessed | tf_op | source)
XLA Modules:
  0.0 60.0 jit_solution(6634272156051650933)
XLA Ops:
  0.0 54.5 %scan.1 = (bf16[1024,2048]{1,0:T(8,128)(2,1)}, f32[8,1024]{1,0:T(8,128)}) custom-call(bf16[1024,2048]{1,0:T(8,128)(2,1)} %x_hbm.1, bf16[1024,512]{1,0:T(8,128)(2,1)} %bc_hbm.1, bf16[1024,2048]{1,0:T(8,128)(2,1)} %z_hbm.1, bf16[32,1024]{1,0:T(8,128)(2,1)} %dt_ref.1, bf16[4,2048]{1,0:T(4,128)(2,1)} %weight_x.1, bf16[4,512]{1,0:T(4,128)(2,1)} %weight_bc.1, ...), custom_call_target="tpu_custom_call" | custom-call | tf_op jit(solution)/shard_map/scan/pallas_call | solution.py:532
  54.5 5.5 %scale.1 = bf16[1024,2048]{1,0:T(8,128)(2,1)} custom-call(bf16[1024,2048]{1,0:T(8,128)(2,1)} %get-tuple-element.7.gated_ref, f32[8,1024]{1,0:T(8,128)} %get-tuple-element.8.factor_ref, f32[1,2048]{1,0:T(1,128)} %bitcast.7), custom_call_target="tpu_custom_call" | custom-call | tf_op jit(solution)/shard_map/scale/pallas_call | solution.py:596

commit v3 on v2

--- a/solution.py
+++ b/solution.py
@@ -27,12 +27,19 @@
     return half + half * jnp.tanh(half)
 
 
-def conv_piece(buffer, row, lanes, taps):
+def conv_piece(buffer, row, lanes, taps, shifted):
     raw = buffer[pl.ds(row, PIECE + RIM), lanes].astype(F32)
-    total = raw[RIM - 3 : RIM - 3 + PIECE] * taps[0:1, lanes] + taps[4:5, lanes]
-    for k in range(1, 4):
-        total = total + raw[RIM - 3 + k : RIM - 3 + k + PIECE] * taps[k : k + 1, lanes]
-    return silu(total).astype(BF16)
+    bias = taps[4:5, lanes]
+    pieces = []
+    for i in range(LANES // 128):
+        part = slice(i * 128, (i + 1) * 128)
+        shifted[i, :, :] = raw[:, part]
+        total = raw[RIM:, part] * taps[3:4, lanes][:, part] + bias[:, part]
+        for k in range(3):
+            tap = taps[k : k + 1, lanes][:, part]
+            total = total + shifted[i, pl.ds(RIM - 3 + k, PIECE), :] * tap
+        pieces.append(silu(total).astype(BF16))
+    return jnp.concatenate(pieces, 1)
 
 
 def two_rows(row):
@@ -99,6 +106,7 @@
     rs,
     taps_x,
     taps_bc,
+    shifted,
     in_sem,
     out_sem,
     send_sem,
@@ -246,7 +254,9 @@
             row = pl.multiple_of(b * SPAN + r * PIECE, PIECE)
             for c in range(2 * groups * STATE // LANES):
                 lanes = pl.ds(c * LANES, LANES)
-                bcc[pl.ds(row, PIECE), lanes] = conv_piece(bcb, row, lanes, taps_bc)
+                bcc[pl.ds(row, PIECE), lanes] = conv_piece(
+                    bcb, row, lanes, taps_bc, shifted.at[c % 2]
+                )
             return carry
 
         if stage == 0:
@@ -257,7 +267,7 @@
             scale = jnp.dot(tt[rows_of(b), :], rn[:, lanes], preferred_element_type=F32)
             for r in range(SPAN // PIECE):
                 row = b * SPAN + r * PIECE
-                conv = conv_piece(xb, row, lanes, taps_x)
+                conv = conv_piece(xb, row, lanes, taps_x, shifted.at[r % 2])
                 xc[pl.ds(row, PIECE), lanes] = conv
                 xp[pl.ds(row, PIECE), lanes] = (
                     conv.astype(F32) * scale[r * PIECE : (r + 1) * PIECE]
@@ -571,6 +581,7 @@
             pltpu.VMEM((n_tp - 1, 8, tokens), F32),
             pltpu.VMEM((8, width), F32),
             pltpu.VMEM((8, bc_width), F32),
+            pltpu.VMEM((2, LANES // 128, PIECE + RIM, 128), F32),
             pltpu.SemaphoreType.DMA((3, blocks)),
             pltpu.SemaphoreType.DMA((blocks,)),
             pltpu.SemaphoreType.DMA((copies,)),
@@ -595,14 +606,14 @@
     )
     return pl.pallas_call(
         scale_kernel,
-        grid=(blocks,),
+        grid=(2 * blocks,),
         out_shape=jax.ShapeDtypeStruct((tokens, width), BF16),
         in_specs=[
-            pl.BlockSpec((SPAN, width), lambda i: (i, 0)),
-            pl.BlockSpec((8, SPAN), lambda i: (0, i)),
+            pl.BlockSpec((SPAN // 2, width), lambda i: (i, 0)),
+            pl.BlockSpec((8, SPAN // 2), lambda i: (0, i)),
             pl.BlockSpec((1, width), lambda i: (0, 0)),
         ],
-        out_specs=pl.BlockSpec((SPAN, width), lambda i: (i, 0)),
+        out_specs=pl.BlockSpec((SPAN // 2, width), lambda i: (i, 0)),
         name="scale",
     )(gated, factor, norm_gain[None, :])
 

time: 60.2 us -> 57.1 us (0.949)
  Pallas kernels: 60 us -> 56.8 us
    pallas_call x1, Pallas kernels: 54.5 us -> 49.3 us  [local(): pl.pallas_call(functools.partial(scan_kernel, n_seq, n_tp, steps), out_sh...]
    pallas_call x1, Pallas kernels: 5.49 us -> 7.44 us  [local(): pl.pallas_call(scale_kernel, grid=(2 * blocks,), out_shape=jax.ShapeDtype...]
where the time goes in v3:
time: 57.1 us; the launch traced here: 56.8 us
  Pallas kernels  56.8 us (99%)
    pallas_call x1, Pallas kernels, local(): pl.pallas_call(functools.partial(scan_kernel, n_seq, n_tp, steps), out_sh...  49.3 us
    pallas_call x1, Pallas kernels, local(): pl.pallas_call(scale_kernel, grid=(2 * blocks,), out_shape=jax.ShapeDtype...  7.44 us

profile of v3, /device:TPU:0, one launch (start us, length us, event | category | flops | bytes accessed | tf_op | source)
XLA Modules:
  0.0 56.8 jit_solution(9832528244386676895)
XLA Ops:
  0.0 49.3 %scan.1 = (bf16[1024,2048]{1,0:T(8,128)(2,1)}, f32[8,1024]{1,0:T(8,128)}) custom-call(bf16[1024,2048]{1,0:T(8,128)(2,1)} %x_hbm.1, bf16[1024,512]{1,0:T(8,128)(2,1)} %bc_hbm.1, bf16[1024,2048]{1,0:T(8,128)(2,1)} %z_hbm.1, bf16[32,1024]{1,0:T(8,128)(2,1)} %dt_ref.1, bf16[4,2048]{1,0:T(4,128)(2,1)} %weight_x.1, bf16[4,512]{1,0:T(4,128)(2,1)} %weight_bc.1, ...), custom_call_target="tpu_custom_call" | custom-call | tf_op jit(solution)/shard_map/scan/pallas_call | solution.py:542
  49.3 7.4 %scale.1 = bf16[1024,2048]{1,0:T(8,128)(2,1)} custom-call(bf16[1024,2048]{1,0:T(8,128)(2,1)} %get-tuple-element.7.gated_ref, f32[8,1024]{1,0:T(8,128)} %get-tuple-element.8.factor_ref, f32[1,2048]{1,0:T(1,128)} %bitcast.7), custom_call_target="tpu_custom_call" | custom-call | tf_op jit(solution)/shard_map/scale/pallas_call | solution.py:607
